TPU v7x, 32 devices: a whole 2x2x4 slice. The times are simulated.
32 devices in a mesh: row: 8 (over z, y), col: 4 (over x, core).
Axes of the slice: x: 2, y: 2, z: 4, core: 2. Of those that a mesh axis runs over, the one named last changes fastest.
Arguments:
- rhs: float32 [65536, 256], P(('row', 'col')), may hold values from -6 to 6
- block_target: int32 [512], P(('row', 'col')), may hold values from 0 to 127, as said below
- pivot_inverse: float32 [32768, 1024], P(('row', 'col')), may hold values from -0.25 to 3, as said below
- update_factor: float32 [32768, 1024], P(('row', 'col')), may hold values from -0.1875 to 0.1875
- root_inverse: float32 [4096, 4096], P('row', 'col'), may hold values from -0.25 to 3, as said below
- update_map: int32 [256], P(('row', 'col')), may hold values from 0 to 31
Outputs:
- front_solution: float32 [32768, 256], P(('row', 'col'))
- root_solution: float32 [4096, 256], P(('row', 'col'))
Inputs may be any that keep to these rules, and one draw needn't show every extreme that they name: block_target[g] is e * 16 + s: block g goes to the device of row index e in its own column, slot s there. Each device sends exactly 2 blocks to each of 8 devices of its column and none to the others; every slot of every device is filled exactly once. `pivot_inverse`: each device's block of 1024 rows is lower triangular with its diagonal positive. `root_inverse`: lower triangular with its diagonal positive.
All inputs are finite; a program needn't handle non-finite values.
Results may differ from a plain program's by a relative error of at most 0.000073.
Values sent between devices are 32-bit elements; how exact they have to be, the bound alone decides.
A program may use at most 192 MiB of HBM per device.

v0:
```python
import jax
import jax.numpy as jnp
from jax import lax
from jax.sharding import PartitionSpec as P

BLK = 128
NRHS = 256
RB_DEV = 16
CAP = 2


def shards(rhs, block_target, pivot_inverse, update_factor, root_inverse, update_map):
    row_count = lax.axis_size("row")
    target_row = block_target // RB_DEV
    slot_index = block_target % RB_DEV
    same_peer = target_row[:, None] == target_row[None, :]
    earlier = lax.broadcasted_iota(jnp.int32, (RB_DEV, RB_DEV), 1) < lax.broadcasted_iota(
        jnp.int32, (RB_DEV, RB_DEV), 0
    )
    peer_rank = jnp.sum(jnp.logical_and(same_peer, earlier), axis=1)
    position = target_row * CAP + peer_rank
    flat_rhs = rhs.reshape(RB_DEV, BLK * NRHS)
    outgoing = jnp.zeros((row_count * CAP, BLK * NRHS), jnp.float32).at[position].set(flat_rhs)
    outgoing_slots = jnp.full((row_count * CAP,), -1, jnp.int32).at[position].set(slot_index)
    arrived, arrived_slots = (
        lax.all_to_all(
            outgoing.reshape(row_count, CAP, BLK * NRHS),
            "row",
            split_axis=0,
            concat_axis=0,
            tiled=True,
        ),
        lax.all_to_all(
            outgoing_slots.reshape(row_count, CAP), "row", split_axis=0, concat_axis=0, tiled=True
        ),
    )
    slot_list = arrived_slots.reshape(-1)
    placement_index = jnp.where(slot_list >= 0, slot_list, RB_DEV)
    front_blocks = (
        jnp.zeros((RB_DEV + 1, BLK * NRHS), jnp.float32)
        .at[placement_index]
        .set(arrived.reshape(row_count * CAP, BLK * NRHS))
    )
    front_rhs = front_blocks[:RB_DEV].reshape(RB_DEV * BLK, NRHS)
    pivot_rows = pivot_inverse.shape[0]
    solved = jnp.dot(
        pivot_inverse,
        front_rhs[:pivot_rows],
        precision=lax.Precision.HIGHEST,
        preferred_element_type=jnp.float32,
    )
    updated = front_rhs[pivot_rows:] - jnp.dot(
        update_factor, solved, precision=lax.Precision.HIGHEST, preferred_element_type=jnp.float32
    )
    update_blocks = updated.reshape(-1, BLK, NRHS)
    all_blocks, all_targets = (
        lax.all_gather(update_blocks, "col", axis=0, tiled=True),
        lax.all_gather(update_map, "col", axis=0, tiled=True),
    )
    col_here = lax.axis_index("col")
    mine = all_targets // row_count == col_here
    local_index = jnp.where(mine, all_targets % row_count, row_count)
    column_part = (
        jnp.zeros((row_count, BLK, NRHS), jnp.float32).at[local_index].add(all_blocks, mode="drop")
    )
    root_piece = lax.psum_scatter(
        column_part.reshape(row_count * BLK, NRHS), "row", scatter_dimension=0, tiled=True
    )
    partial_value = jnp.dot(
        root_inverse,
        lax.all_gather(root_piece, "row", axis=0, tiled=True),
        precision=lax.Precision.HIGHEST,
        preferred_element_type=jnp.float32,
    )
    root_solution = lax.psum_scatter(partial_value, "col", scatter_dimension=0, tiled=True)
    return (solved, root_solution)


def solution(mesh):
    return jax.shard_map(
        shards,
        mesh=mesh,
        in_specs=(
            P(("row", "col"), None),
            P(("row", "col")),
            P(("row", "col"), None),
            P(("row", "col"), None),
            P("row", "col"),
            P(("row", "col")),
        ),
        out_specs=(P(("row", "col"), None), P(("row", "col"), None)),
        check_vma=False,
    )
```

profile of v0, /device:TPU:1, one launch (start us, length us, event | category | flops | bytes accessed | tf_op | source)
XLA Modules:
  0.0 294.7 jit_solution(12418113078786546350)
XLA Ops:
  7.2 0.0 copy-start
  7.2 0.8 and_select_fusion.2
  8.0 0.2 convert_reduce_fusion
  8.2 0.6 scatter_custom_fusion
  8.8 0.7 all_to_all.9
  9.5 6.4 %all-to-all-start = ((s32[8,1,2]{2,1,0:T(1,128)}), s32[8,1,2]{2,1,0:T(1,128)S(1)}, u32[]{:S(2)}, u32[]{:S(2)}) async-start(s32[8,1,2]{2,1,0:T(1,128)} %bitcast), calls=%async_computation | async-start | bytes 8192 | tf_op jit(solution)/shard_map/all_to_all | solution.py:33
  15.9 2.7 reshape.78
  18.6 4.2 %scatter_custom_fusion.1 = f32[16,32768]{1,0:T(8,128)} fusion(s32[16]{0:T(128)S(1)} %compare_select_fusion.3, f32[16,32768]{1,0:T(8,128)} %reshape.78, f32[]{:T(128)} %constant.58.clone.1), kind=kCustom, calls=%fused_computation.9 | custom fusion | bytes 2097664 | tf_op jit(solution)/shard_map/scatter | solution.py:23
  22.8 3.5 %reshape.62 = f32[8,2,32768]{2,1,0:T(2,128)} reshape(f32[16,32768]{1,0:T(8,128)} %scatter_custom_fusion.1) | data formatting | bytes 4194304 | tf_op jit(solution)/shard_map/reshape | solution.py:27
  26.2 0.0 all-to-all-done
  26.2 5.4 %all-to-all-start.1 = ((f32[8,2,32768]{2,1,0:T(2,128)}), f32[8,2,32768]{2,1,0:T(2,128)}, u32[]{:S(2)}, u32[]{:S(2)}) async-start(f32[8,2,32768]{2,1,0:T(2,128)} %reshape.62), calls=%async_computation.1 | async-start | bytes 4194304 | tf_op jit(solution)/shard_map/all_to_all | solution.py:26
  31.6 0.0 all-gather.3.cloned.1.call-start
  31.7 0.5 broadcast.95
  32.2 0.7 reduce.3
  32.9 0.1 reshape.60
  33.0 45.7 %all-to-all-done.1 = f32[8,2,32768]{2,1,0:T(2,128)} async-done(((f32[8,2,32768]{2,1,0:T(2,128)}), f32[8,2,32768]{2,1,0:T(2,128)}, u32[]{:S(2)}, u32[]{:S(2)}) %all-to-all-start.1) | async-done | bytes 2097184 | tf_op jit(solution)/shard_map/all_to_all | solution.py:26
  78.6 3.6 %reshape.86 = f32[16,32768]{1,0:T(8,128)} reshape(f32[8,2,32768]{2,1,0:T(2,128)} %all-to-all-done.1) | data formatting | bytes 4194304 | tf_op jit(solution)/shard_map/reshape | solution.py:42
  82.3 4.6 %scatter_custom_fusion.2 = f32[17,32768]{1,0:T(8,128)} fusion(s32[16]{0:T(128)S(1)} %fusion.6, f32[16,32768]{1,0:T(8,128)} %reshape.86, f32[]{:T(128)} %constant.58.clone.1), kind=kCustom, calls=%fused_computation.4 | custom fusion | bytes 2228736 | tf_op jit(solution)/shard_map/scatter | solution.py:42
  86.8 2.6 fusion.9
  89.5 2.4 slice.16
  91.8 1.1 slice.18
  93.0 1.6 copy.20
  94.5 0.0 copy-start.4
  94.5 9.1 %fusion.10 = f32[256,1024]{1,0:T(8,128)S(1)} fusion(f32[1024,256]{1,0:T(8,128)} %slice.16, f32[1024,1024]{1,0:T(8,128)} %param.8), kind=kOutput, calls=%fused_computation.33 | convolution fusion | flops 3221225472 | bytes 6291456 | tf_op jit(solution)/shard_map/dot_general | solution.py:46
  103.7 0.0 copy-start.2
  103.7 1.0 copy-done.2
  104.7 0.0 copy-done.4
  104.7 4.7 %fusion.2 = f32[1024,256]{0,1:T(8,128)} fusion(f32[1024,256]{0,1:T(8,128)S(1)} %copy.20, f32[256,1024]{1,0:T(8,128)S(1)} %fusion.10, f32[1024,1024]{1,0:T(8,128)S(1)} %copy-done.4), kind=kOutput, calls=%fused_computation.7 | convolution fusion | flops 3221487616 | bytes 7340032 | tf_op jit(solution)/shard_map/dot_general | solution.py:52
  109.4 0.0 copy-start.6
  109.4 0.0 copy-start.5
  109.4 2.6 copy.24
  111.9 0.0 all-gather.3.cloned.1.call-update
  111.9 0.0 reduce-scatter.3.cloned.1.call-start
  112.0 0.0 copy-done.6
  112.0 0.6 dynamic-slice
  113.3 0.0 copy-done.5
  113.3 0.2 dynamic-update-slice
  113.5 5.9 %all-reduce = s32[32]{0:T(128)S(1)} all-reduce(s32[32]{0:T(128)S(1)} %dynamic-update-slice), channel_id=1, replica_groups=mesh['row'=8,'col'=4] {'col'}, use_global_device_ids=true, to_apply=%add | all-reduce | flops 32 | bytes 256
  119.4 28.3 %all-gather.3.cloned.1.call-done = f32[32,128,256]{2,1,0:T(8,128)} async-done(((f32[8,128,256]{2,1,0:T(8,128)}), f32[32,128,256]{2,1,0:T(8,128)}) %all-gather.3.cloned.1.call-update) | async-done | bytes 4194320 | tf_op jit(solution)/shard_map/all_gather | solution.py:57
  147.7 0.1 broadcast_in_dim.26
  147.7 6.4 %scatter_fusion = f32[8,128,256]{2,1,0:T(8,128)S(1)} fusion(f32[8,128,256]{2,1,0:T(8,128)S(1)} %broadcast_in_dim.26, s32[32]{0:T(128)S(1)} %compare_select_fusion, f32[32,128,256]{2,1,0:T(8,128)} %all-gather.3.cloned.1.call-done), kind=kCustom, calls=%fused_computation.3 | custom fusion | flops 1048576 | bytes 12583040 | tf_op jit(solution)/shard_map/scatter-add | solution.py:64
  154.2 0.0 copy-start.1
  154.2 1.0 copy-done.1
  155.2 0.0 reduce-scatter.3.cloned.1.call-update
  155.2 0.0 all-gather.5.cloned.1.call-start
  155.2 62.1 %reduce-scatter.3.cloned.1.call-done = f32[128,256]{1,0:T(8,128)} async-done(((f32[1024,256]{1,0:T(8,128)}), f32[128,256]{1,0:T(8,128)}) %reduce-scatter.3.cloned.1.call-update) | async-done | bytes 131088 | tf_op jit(solution)/shard_map/reduce_scatter | solution.py:66
  217.3 0.0 all-gather.5.cloned.1.call-update
  217.3 0.0 copy-start.3
  217.4 0.3 reduce-scatter.5.cloned.1.call-start
  217.6 41.2 %all-gather.5.cloned.1.call-done = f32[1024,256]{1,0:T(8,128)} async-done(((f32[128,256]{1,0:T(8,128)}), f32[1024,256]{1,0:T(8,128)}) %all-gather.5.cloned.1.call-update) | async-done | bytes 1048592 | tf_op jit(solution)/shard_map/all_gather | solution.py:71
  258.9 0.0 copy-done
  258.9 5.6 %convolution_bitcast_fusion.1 = f32[512,256]{0,1:T(8,128)} fusion(f32[1024,256]{1,0:T(8,128)} %all-gather.5.cloned.1.call-done, f32[512,1024]{1,0:T(8,128)S(1)} %copy-done), kind=kOutput, calls=%fused_computation.8 | convolution fusion | flops 1610612736 | bytes 3670016 | tf_op jit(solution)/shard_map/dot_general | solution.py:69
  264.4 0.0 reduce-scatter.5.cloned.1.call-update
  264.4 0.0 copy-done.3
  264.5 1.3 copy.22
  265.8 20.7 %reduce-scatter.5.cloned.1.call-done = f32[128,256]{0,1:T(8,128)} async-done(((f32[512,256]{0,1:T(8,128)}), f32[128,256]{0,1:T(8,128)}) %reduce-scatter.5.cloned.1.call-update) | async-done | bytes 131088 | tf_op jit(solution)/shard_map/reduce_scatter | solution.py:75
  286.5 1.7 copy.23
  (4 shorter events, 0.0 us)
Async XLA Ops:
  7.2 251.7 %copy-start = (f32[512,1024]{1,0:T(8,128)S(1)}, f32[512,1024]{1,0:T(8,128)}, u32[]{:S(2)}) copy-start(f32[512,1024]{1,0:T(8,128)} %param.10) | copy-start | bytes 6291460
  9.5 16.7 %all-to-all-start = ((s32[8,1,2]{2,1,0:T(1,128)}), s32[8,1,2]{2,1,0:T(1,128)S(1)}, u32[]{:S(2)}, u32[]{:S(2)}) async-start(s32[8,1,2]{2,1,0:T(1,128)} %bitcast), calls=%async_computation | async-start | bytes 8192 | tf_op jit(solution)/shard_map/all_to_all | solution.py:33
  26.2 52.4 %all-to-all-start.1 = ((f32[8,2,32768]{2,1,0:T(2,128)}), f32[8,2,32768]{2,1,0:T(2,128)}, u32[]{:S(2)}, u32[]{:S(2)}) async-start(f32[8,2,32768]{2,1,0:T(2,128)} %reshape.62), calls=%async_computation.1 | async-start | bytes 4194304 | tf_op jit(solution)/shard_map/all_to_all | solution.py:26
  31.6 116.0 %all-gather.3.cloned.1.call-start = ((), (), s32[]{:S(2)}) async-start(), calls=%async_computation.4 | async-start | bytes 5242880 | tf_op jit(solution)/shard_map/all_gather | solution.py:57
  94.5 10.1 %copy-start.4 = (f32[1024,1024]{1,0:T(8,128)S(1)}, f32[1024,1024]{1,0:T(8,128)}, u32[]{:S(2)}) copy-start(f32[1024,1024]{1,0:T(8,128)} %param.9) | copy-start | bytes 12582916
  103.7 1.0 copy-start.2
  109.4 2.6 copy-start.6
  109.4 3.9 %copy-start.5 = (s32[8]{0:T(128)S(1)}, s32[8]{0:T(128)}, u32[]{:S(2)}) copy-start(s32[8]{0:T(128)} %param.11) | copy-start | bytes 100
  111.9 105.4 %reduce-scatter.3.cloned.1.call-start = ((), (), s32[]{:S(2)}) async-start(), calls=%async_computation.5 | async-start | bytes 1179648 | tf_op jit(solution)/shard_map/reduce_scatter | solution.py:66
  154.2 1.0 copy-start.1
  155.2 103.7 %all-gather.5.cloned.1.call-start = ((), (), s32[]{:S(2)}) async-start(), calls=%async_computation.6 | async-start | bytes 1179648 | tf_op jit(solution)/shard_map/all_gather | solution.py:71
  217.3 47.1 %copy-start.3 = (f32[256,1024]{1,0:T(8,128)S(1)}, f32[256,1024]{1,0:T(8,128)}, u32[]{:S(2)}) copy-start(f32[256,1024]{1,0:T(8,128)} %copy-done.2) | copy-start | bytes 3145732
  217.4 69.2 %reduce-scatter.5.cloned.1.call-start = ((), (), s32[]{:S(2)}) async-start(), calls=%async_computation.7 | async-start | bytes 655360 | tf_op jit(solution)/shard_map/reduce_scatter | solution.py:75
Sparse Core Ops, SparseCore 0:
  112.1 35.5 all-gather.2
  155.3 61.9 reduce-scatter.2
  219.4 39.3 all-gather.4
  264.6 21.8 reduce-scatter.4
where the time goes:
time: 296 us; the launch traced here: 295 us
  waiting for transfers between devices  198 us (67%)
  local copies, waits for them, and re-layouts  36.5 us (12%)
  matrix products  19.4 us (7%)
  between operations  14.6 us (5%)
  starting transfers between devices  12.2 us (4%)
  other arithmetic  8.12 us (3%)
  blocking collectives  5.87 us (2%)
    reduce_scatter x1, waiting for transfers between devices, shards(): lax.psum_scatter(column_part.reshape(row_count * BLK, NRHS), 'row', scatt...  62.1 us
    all_to_all x1, waiting for transfers between devices, shards(): lax.all_to_all(outgoing.reshape(row_count, CAP, BLK * NRHS), 'row', split...  45.7 us
    all_gather x1, waiting for transfers between devices, shards(): lax.all_gather(root_piece, 'row', axis=0, tiled=True)  41.2 us
    all_gather x1, waiting for transfers between devices, shards(): lax.all_gather(update_blocks, 'col', axis=0, tiled=True)  28.3 us
    reduce_scatter x1, waiting for transfers between devices, shards(): lax.psum_scatter(partial_value, 'col', scatter_dimension=0, tiled=True)  20.7 us
    dot_general x1, matrix products, shards(): jnp.dot(pivot_inverse, front_rhs[:pivot_rows], precision=lax.Precision.HI...  9.15 us
    scatter-add x1, other arithmetic, shards(): jnp.zeros((row_count, BLK, NRHS), jnp.float32).at[local_index]  6.43 us
    all_to_all x1, starting transfers between devices, shards(): lax.all_to_all(outgoing_slots.reshape(row_count, CAP), 'row', split_axis=...  6.37 us
  transfers between devices with their start and end apart: 6, of which 5 were waited for; matrix products, arithmetic and copies ran while one was open for 5% of the time, Pallas kernels for 0%

commit v1 on v0

v1 whole, which is shorter than its diff:
```python
import functools
import jax
import jax.numpy as jnp
from jax import lax
from jax.experimental import pallas as pl
from jax.experimental.pallas import tpu as pltpu
from jax.sharding import PartitionSpec as P

BLK = 128
CAP = 2
CHUNKS = 16
MESH = pl.DeviceIdType.MESH
VMEM = pl.BlockSpec(memory_space=pltpu.VMEM)
SMEM = pl.BlockSpec(memory_space=pltpu.SMEM)


def split(value):
    high = value.astype(jnp.bfloat16)
    low = (value - high.astype(jnp.float32)).astype(jnp.bfloat16)
    return high, low


def dot3(a, b_high, b_low):
    a_high, a_low = split(a)
    total = jnp.dot(a_high, b_low, preferred_element_type=jnp.float32)
    total += jnp.dot(a_low, b_high, preferred_element_type=jnp.float32)
    return total + jnp.dot(a_high, b_high, preferred_element_type=jnp.float32)


def exchange_kernel(n_row, order, target_ref, rhs_ref, arrived, slots, staging, messages, send, recv, send_int, recv_int):
    me, col = lax.axis_index("row"), lax.axis_index("col")
    held = rhs_ref.shape[0]
    barrier = pltpu.get_barrier_semaphore()
    for k in order:
        pl.semaphore_signal(barrier, inc=1, device_id=(me ^ k, col), device_id_type=MESH)
    lane = lax.broadcasted_iota(jnp.int32, (8, 128), 1)
    targets = [target_ref[g] for g in range(held)]

    def chosen(peer):
        first, last = jnp.int32(held), jnp.int32(-1)
        slot_first, slot_last = jnp.int32(-1), jnp.int32(-1)
        for g in range(held):
            match = lax.div(targets[g], held) == peer
            fresh = jnp.logical_and(match, last < 0)
            first = jnp.where(fresh, g, first)
            slot_first = jnp.where(fresh, lax.rem(targets[g], held), slot_first)
            last = jnp.where(match, g, last)
            slot_last = jnp.where(match, lax.rem(targets[g], held), slot_last)
        return (
            jnp.minimum(first, held - 1),
            jnp.maximum(last, 0),
            jnp.where(lane == 0, slot_first, slot_last),
        )

    def stage(ref, place, peer):
        first, last, row = chosen(peer)
        ref[place, 0:BLK] = rhs_ref[first]
        ref[place, BLK : 2 * BLK] = rhs_ref[last]
        return row

    copies = []
    for place, k in enumerate(order):
        messages[place] = stage(staging, place, me ^ k)
        if place == 0:
            pl.semaphore_wait(barrier, n_row - 1)
        for source, target, ss, rs in (
            (staging, arrived, send, recv),
            (messages, slots, send_int, recv_int),
        ):
            copy = pltpu.make_async_remote_copy(
                src_ref=source.at[place],
                dst_ref=target.at[me],
                send_sem=ss.at[place],
                recv_sem=rs.at[place],
                device_id=(me ^ k, col),
                device_id_type=MESH,
            )
            copy.start()
            copies.append(copy)
    slots[me] = stage(arrived, me, me)
    for copy in copies:
        copy.wait()


def front_kernel(n_row, root_blocks, arrived, slots, update_map, pivot, factor, solved, dense, inverse, high, low):
    held = arrived.shape[0]
    rows = pivot.shape[0]
    tile = 2 * BLK
    half = rows // BLK
    for s in range(n_row):
        for rank in range(CAP):
            slot = slots[s, 0, rank]

            @pl.when(slot >= 0)
            def _():
                inverse[slot] = s * CAP + rank

    for b in range(half):
        part = pl.ds(b * BLK, BLK)
        high[part], low[part] = split(arrived[inverse[b]])

    @pl.loop(0, root_blocks)
    def _(b):
        dense[b] = jnp.zeros_like(dense[b])

    for start in range(0, rows, tile):
        deep = start + tile
        solved[start : start + tile] = dot3(pivot[start : start + tile, :deep], high[:deep], low[:deep])
    for start in range(0, rows, tile):
        part = pl.ds(start, tile)
        high[part], low[part] = split(solved[part])
    for start in range(0, rows, tile):
        product = dot3(factor[start : start + tile], high[...], low[...])
        for step in range(tile // BLK):
            b = start // BLK + step
            value = arrived[inverse[half + b]] - product[step * BLK : (step + 1) * BLK]
            dense[update_map[b]] += value


def root_kernel(
    n_row, n_col, skew, dense, inverse, out,
    got_core, got_x, y_up, y_down, y_us, y_ds, mid, z_up, z_down, z_us, z_ds,
    high, low, product, got_col,
    core_send, core_recv, x_send, x_recv, y_send, y_recv, z_send, z_recv, col_send, col_recv,
):
    n_y = max(1, n_col // 2)
    n_z, n_x = n_row // n_y, n_col // 2
    r, c = lax.axis_index("row"), lax.axis_index("col")
    z, y, x, k = r // n_y, r % n_y, c // 2, c % 2
    size = n_row * BLK
    step_rows = size // CHUNKS

    barrier = pltpu.get_barrier_semaphore()

    def greet(device):
        pl.semaphore_signal(barrier, inc=1, device_id=device, device_id_type=MESH)

    for d in range(1, n_col):
        greet((r, (c + d) % n_col))
    for pos, n, stride in ((y, n_y, 1), (z, n_z, n_y)):
        pl.when(pos > 0)(functools.partial(greet, (r - stride, c)))
        pl.when(pos < n - 1)(functools.partial(greet, (r + stride, c)))
    count = n_col - 1
    for pos, n in ((y, n_y), (z, n_z)):
        count = count + jnp.where(pos > 0, 1, 0) + jnp.where(pos < n - 1, 1, 0)
    pl.semaphore_wait(barrier, count)

    def remote(src, dst, ss, rs, device):
        return pltpu.make_async_remote_copy(
            src_ref=src, dst_ref=dst, send_sem=ss, recv_sem=rs, device_id=device, device_id_type=MESH
        )

    def rows_of(i):
        return pl.ds(pl.multiple_of(i * step_rows, step_rows), step_rows)

    def dense_rows(column, i):
        return pl.ds(pl.multiple_of(column * size + i * step_rows, step_rows), step_rows)

    partner = (r, c - k + (1 - k))
    base = got_core.at[0]

    def core_copy(d, i):
        xx = (x + d) % n_x
        return remote(
            dense.at[dense_rows(2 * xx + (1 - k), i)],
            got_core.at[d, rows_of(i)],
            core_send.at[d],
            core_recv.at[d, i],
            partner,
        )

    @pl.loop(0, CHUNKS)
    def _(i):
        for d in range(n_x - 1, -1, -1):
            core_copy(d, i).start()

    def x_copy(d, i):
        return remote(
            got_core.at[d, rows_of(i)],
            got_x.at[d - 1, rows_of(i)],
            x_send.at[d - 1],
            x_recv.at[d - 1, i],
            (r, ((x + d) % n_x) * 2 + k),
        )

    def stage_x(i):
        for d in range(n_x - 1, -1, -1):
            xx = (x + d) % n_x
            core_copy(d, i).wait_recv()
            value = dense[dense_rows(2 * xx + k, i)] + got_core[d, rows_of(i)]
            got_core[d, rows_of(i)] = value
            if d:
                x_copy(d, i).start()

    def join_x(i):
        value = base[rows_of(i)]
        for d in range(1, n_x):
            x_copy(d, i).wait_recv()
            value = value + got_x[d - 1, rows_of(i)]
        base[rows_of(i)] = value

    def line(n, pos, stride, held, up, down, us, ds, ss, rs):
        def send_up(i, source):
            return remote(source.at[rows_of(i)], up.at[rows_of(i)], ss.at[0], rs.at[0, i], (r + stride, c))

        def send_down(i, source):
            return remote(source.at[rows_of(i)], down.at[rows_of(i)], ss.at[1], rs.at[1, i], (r - stride, c))

        def hop(h, i):
            for place, landed, total, send in (
                (pos, up, us, send_up),
                (n - 1 - pos, down, ds, send_down),
            ):
                @pl.when(place == h)
                def _():
                    if h == 0:
                        send(i, held).start()
                    else:
                        send(i, total).wait_recv()
                        if h < n - 1:
                            total[rows_of(i)] = held[rows_of(i)] + landed[rows_of(i)]
                            send(i, total).start()

        def total(i, write):
            part = rows_of(i)

            @pl.when(pos == 0)
            def _():
                write(part, held[part] + down[part])

            @pl.when(pos == n - 1)
            def _():
                write(part, held[part] + up[part])

            if n > 2:
                @pl.when(jnp.logical_and(pos > 0, pos < n - 1))
                def _():
                    write(part, held[part] + up[part] + down[part])

        def drain():
            whole = pl.ds(0, size)

            @pl.when(pos < n - 1)
            def _():
                remote(held.at[whole], up.at[whole], ss.at[0], rs.at[0, 0], (r + stride, c)).wait_send()

            @pl.when(pos > 0)
            def _():
                remote(held.at[whole], down.at[whole], ss.at[1], rs.at[1, 0], (r - stride, c)).wait_send()

        return hop, total, drain

    y_hop, y_total, y_drain = line(n_y, y, 1, base, y_up, y_down, y_us, y_ds, y_send, y_recv)
    z_hop, z_total, z_drain = line(n_z, z, n_y, mid, z_up, z_down, z_us, z_ds, z_send, z_recv)

    def write_mid(part, value):
        mid[part] = value

    def write_split(part, value):
        high[part], low[part] = split(value)

    stages = [(0, stage_x)]
    at = skew

    def y_first(i):
        join_x(i)
        y_hop(0, i)

    stages.append((at, y_first))
    for h in range(1, n_y):
        at += skew
        if h < n_y - 1:
            stages.append((at, functools.partial(y_hop, h)))

    def z_first(i):
        y_hop(n_y - 1, i)
        y_total(i, write_mid)
        z_hop(0, i)

    stages.append((at, z_first))
    for h in range(1, n_z):
        at += skew
        if h < n_z - 1:
            stages.append((at, functools.partial(z_hop, h)))

    def z_last(i):
        z_hop(n_z - 1, i)
        z_total(i, write_split)

    stages.append((at, z_last))

    @pl.loop(0, CHUNKS + at)
    def _(t):
        for offset, stage in stages:
            i = t - offset

            @pl.when(jnp.logical_and(i >= 0, i < CHUNKS))
            def _():
                stage(i)

    tile = 2 * BLK
    for start in range(0, n_col * BLK, tile):
        product[start : start + tile] = dot3(inverse[start : start + tile], high[...], low[...])

    def col_copy(d):
        to = (c + d) % n_col
        return remote(
            product.at[pl.ds(pl.multiple_of(to * BLK, BLK), BLK)],
            got_col.at[d - 1],
            col_send.at[d - 1],
            col_recv.at[d - 1],
            (r, to),
        )

    for d in range(1, n_col):
        col_copy(d).start()
    value = product[pl.ds(pl.multiple_of(c * BLK, BLK), BLK)]
    for d in range(1, n_col):
        col_copy(d).wait_recv()
        value = value + got_col[d - 1]
    out[...] = value

    for d in range(1, n_col):
        col_copy(d).wait_send()
    for d in range(n_x):
        remote(
            dense.at[pl.ds(0, size)], got_core.at[d], core_send.at[d], core_recv.at[d, 0], partner
        ).wait_send()
    for d in range(1, n_x):
        remote(
            got_core.at[d], got_x.at[d - 1], x_send.at[d - 1], x_recv.at[d - 1, 0],
            (r, ((x + d) % n_x) * 2 + k),
        ).wait_send()
    y_drain()
    z_drain()


def shards(rhs, block_target, pivot_inverse, update_factor, root_inverse, update_map):
    n_row, n_col = lax.axis_size("row"), lax.axis_size("col")
    n_x = n_col // 2
    width = rhs.shape[1]
    held = rhs.shape[0] // BLK
    rows = pivot_inverse.shape[0]
    root_blocks = n_row * n_col
    size = n_row * BLK
    f32 = jnp.float32
    far = [k for k in range(n_row - 1, 0, -1)]
    half = n_row // 2
    near = [k for k in far if 1 < k < half]
    cross = [k for k in far if k >= half]
    order = []
    for place in range(max(len(near), len(cross))):
        order += near[place : place + 1] + cross[place : place + 1]
    order += [1]
    arrived, slots = pl.pallas_call(
        functools.partial(exchange_kernel, n_row, order),
        out_shape=(
            jax.ShapeDtypeStruct((n_row, CAP * BLK, width), f32),
            jax.ShapeDtypeStruct((n_row, 8, 128), jnp.int32),
        ),
        in_specs=[SMEM, VMEM],
        out_specs=(VMEM, VMEM),
        scratch_shapes=[
            pltpu.VMEM((n_row - 1, CAP * BLK, width), f32),
            pltpu.VMEM((n_row - 1, 8, 128), jnp.int32),
        ]
        + [pltpu.SemaphoreType.DMA((n_row - 1,))] * 4,
        compiler_params=pltpu.CompilerParams(collective_id=0, has_side_effects=True),
        name="exchange",
    )(block_target, rhs.reshape(held, BLK, width))
    solved, dense = pl.pallas_call(
        functools.partial(front_kernel, n_row, root_blocks),
        out_shape=(
            jax.ShapeDtypeStruct((rows, width), f32),
            jax.ShapeDtypeStruct((root_blocks, BLK, width), f32),
        ),
        in_specs=[VMEM, SMEM, SMEM, VMEM, VMEM],
        out_specs=(VMEM, VMEM),
        scratch_shapes=[
            pltpu.SMEM((held,), jnp.int32),
            pltpu.VMEM((rows, width), jnp.bfloat16),
            pltpu.VMEM((rows, width), jnp.bfloat16),
        ],
        name="front",
    )(arrived.reshape(n_row * CAP, BLK, width), slots, update_map, pivot_inverse, update_factor)
    slab = pltpu.VMEM((size, width), f32)
    root_solution = pl.pallas_call(
        functools.partial(root_kernel, n_row, n_col, 2),
        out_shape=jax.ShapeDtypeStruct((BLK, width), f32),
        in_specs=[VMEM, VMEM],
        out_specs=VMEM,
        scratch_shapes=[
            pltpu.VMEM((n_x, size, width), f32),
            pltpu.VMEM((n_x - 1, size, width), f32),
        ]
        + [slab] * 9
        + [
            pltpu.VMEM((size, width), jnp.bfloat16),
            pltpu.VMEM((size, width), jnp.bfloat16),
            pltpu.VMEM((n_col * BLK, width), f32),
            pltpu.VMEM((n_col - 1, BLK, width), f32),
            pltpu.SemaphoreType.DMA((n_x,)),
            pltpu.SemaphoreType.DMA((n_x, CHUNKS)),
            pltpu.SemaphoreType.DMA((n_x - 1,)),
            pltpu.SemaphoreType.DMA((n_x - 1, CHUNKS)),
            pltpu.SemaphoreType.DMA((2,)),
            pltpu.SemaphoreType.DMA((2, CHUNKS)),
            pltpu.SemaphoreType.DMA((2,)),
            pltpu.SemaphoreType.DMA((2, CHUNKS)),
            pltpu.SemaphoreType.DMA((n_col - 1,)),
            pltpu.SemaphoreType.DMA((n_col - 1,)),
        ],
        compiler_params=pltpu.CompilerParams(
            collective_id=1, has_side_effects=True, vmem_limit_bytes=67043328
        ),
        name="root",
    )(dense.reshape(root_blocks * BLK, width), root_inverse)
    return (solved, root_solution)


def solution(mesh):
    return jax.shard_map(
        shards,
        mesh=mesh,
        in_specs=(
            P(("row", "col"), None),
            P(("row", "col")),
            P(("row", "col"), None),
            P(("row", "col"), None),
            P("row", "col"),
            P(("row", "col")),
        ),
        out_specs=(P(("row", "col"), None), P(("row", "col"), None)),
        check_vma=False,
    )
```

time: 296 us -> 125 us (0.42)
  waiting for transfers between devices: 198 us -> 0 us
  Pallas kernels: 0 us -> 123 us
  local copies, waits for them, and re-layouts: 36.5 us -> 1.57 us
  matrix products: 19.4 us -> 0 us
  between operations: 14.6 us -> 0.65 us
  starting transfers between devices: 12.2 us -> 0 us
  other arithmetic: 8.12 us -> 0 us
  blocking collectives: 5.87 us -> 0 us
    pallas_call x0 -> x3, Pallas kernels: none -> 123 us  [the longest x1 57.1 us: shards(): pl.pallas_call(functools.partial(exchange_kernel, n_row, order), out_shap...]
    reduce_scatter x2 -> x0, waiting for transfers between devices: 82.8 us -> none  [the longest x1 62.1 us: shards(): lax.psum_scatter(column_part.reshape(row_count * BLK, NRHS), 'row', scatt...]
    all_gather x2 -> x0, waiting for transfers between devices: 69.5 us -> none  [the longest x1 41.2 us: shards(): lax.all_gather(root_piece, 'row', axis=0, tiled=True)]
    all_to_all x2 -> x0, waiting for transfers between devices: 45.7 us -> none  [the longest x1 45.7 us: shards(): lax.all_to_all(outgoing.reshape(row_count, CAP, BLK * NRHS), 'row', split...]
    dot_general x3 -> x0, matrix products: 19.4 us -> none  [the longest x1 9.15 us: shards(): jnp.dot(pivot_inverse, front_rhs[:pivot_rows], precision=lax.Precision.HI...]
    reshape x5 -> x0, local copies, waits for them, and re-layouts: 12.4 us -> none  [the longest x1 3.64 us: shards(): arrived.reshape(row_count * CAP, BLK * NRHS)]
    all_to_all x2 -> x0, starting transfers between devices: 11.8 us -> none  [the longest x1 6.37 us: shards(): lax.all_to_all(outgoing_slots.reshape(row_count, CAP), 'row', split_axis=...]
    scatter x3 -> x0, local copies, waits for them, and re-layouts: 9.35 us -> none  [the longest x1 4.56 us: shards(): front_blocks = jnp.zeros((RB_DEV + 1, BLK * NRHS), jnp.float32).at[placem...]
  transfers between devices with their start and end apart: 6 -> 0, of which waited for: 5 -> 0; matrix products, arithmetic and copies ran while one was open for 5% -> 0% of each run, Pallas kernels for 0% -> 0%
where the time goes in v1:
time: 125 us
  Pallas kernels  123 us (98%)
  local copies, waits for them, and re-layouts  1.57 us (1%)
    pallas_call x1, Pallas kernels, shards(): pl.pallas_call(functools.partial(exchange_kernel, n_row, order), out_shap...  57.1 us
    pallas_call x1, Pallas kernels, shards(): pl.pallas_call(functools.partial(root_kernel, n_row, n_col, 2), out_shape...  56.4 us
    pallas_call x1, Pallas kernels, shards(): pl.pallas_call(functools.partial(front_kernel, n_row, root_blocks), out_s...  9.47 us

profile of v1, /device:TPU:1, one launch (start us, length us, event | category | flops | bytes accessed | tf_op | source)
XLA Modules:
  0.0 125.2 jit_solution(14081664156701460739)
XLA Ops:
  0.6 57.1 %exchange.1 = (f32[8,256,256]{2,1,0:T(8,128)}, s32[8,8,128]{2,1,0:T(8,128)}) custom-call(s32[16]{0:T(128)} %target_ref.1, f32[16,128,256]{2,1,0:T(8,128)} %bitcast.4), custom_call_target="tpu_custom_call" | custom-call | tf_op jit(solution)/shard_map/exchange/pallas_call | solution.py:355
  57.8 9.5 %front.1 = (f32[1024,256]{1,0:T(8,128)}, f32[32,128,256]{2,1,0:T(8,128)}) custom-call(f32[16,128,256]{2,1,0:T(8,128)} %bitcast.5, s32[8,8,128]{2,1,0:T(8,128)} %get-tuple-element.7.slots, s32[8]{0:T(128)} %update_map.1, f32[1024,1024]{1,0:T(8,128)} %pivot.1, f32[1024,1024]{1,0:T(8,128)} %factor.1), custom_call_target="tpu_custom_call" | custom-call | tf_op jit(solution)/shard_map/front/pallas_call | solution.py:371
  67.2 56.4 %root.1 = f32[128,256]{1,0:T(8,128)} custom-call(f32[4096,256]{1,0:T(8,128)} %bitcast.3, f32[512,1024]{1,0:T(8,128)} %inverse.1), custom_call_target="tpu_custom_call" | custom-call | tf_op jit(solution)/shard_map/root/pallas_call | solution.py:387
  123.7 1.6 %copy.9 = f32[128,256]{1,0:T(8,128)} copy(f32[128,256]{1,0:T(8,128)} %root.1) | data formatting | bytes 262144

commit v2 on v1

v2 whole, which is shorter than its diff:
```python
import functools
import jax
import jax.numpy as jnp
from jax import lax
from jax.experimental import pallas as pl
from jax.experimental.pallas import tpu as pltpu
from jax.sharding import PartitionSpec as P

BLK = 128
CAP = 2
CHUNKS = 32
CORE_SKEW = 2
LEAD = 6
SKEW = 4
MESH = pl.DeviceIdType.MESH
VMEM = pl.BlockSpec(memory_space=pltpu.VMEM)
SMEM = pl.BlockSpec(memory_space=pltpu.SMEM)
ANY = pl.BlockSpec(memory_space=pl.ANY)


def split(value):
    high = value.astype(jnp.bfloat16)
    low = (value - high.astype(jnp.float32)).astype(jnp.bfloat16)
    return high, low


def dot3(a, b_high, b_low):
    a_high, a_low = split(a)
    total = jnp.dot(a_high, b_low, preferred_element_type=jnp.float32)
    total += jnp.dot(a_low, b_high, preferred_element_type=jnp.float32)
    return total + jnp.dot(a_high, b_high, preferred_element_type=jnp.float32)


def forward_kernel(
    n_row, n_col, order, target_ref, map_ref, rhs_ref, pivot_hbm, factor_hbm, inverse_hbm,
    solved, out,
    staging, messages, arrived, slots, slots_smem, place_ref, weights, high, low, updated,
    give, got_core, got_x, y_up, y_down, y_ds, mid, z_up, z_down, z_ds, product, got_col,
    weight_sem, slot_sem, send, recv, send_int, recv_int,
    core_send, core_recv, x_send, x_recv, y_send, y_recv, z_send, z_recv, col_send, col_recv,
):
    n_y = max(1, n_col // 2)
    n_z, n_x = n_row // n_y, n_col // 2
    r, c = lax.axis_index("row"), lax.axis_index("col")
    z, y, x, k = r // n_y, r % n_y, c // 2, c % 2
    size = n_row * BLK
    step_rows = size // CHUNKS
    held = rhs_ref.shape[0]
    rows = solved.shape[0]
    half = rows // BLK
    tile = 2 * BLK
    base = got_core.at[0]

    def remote(src, dst, ss, rs, device):
        return pltpu.make_async_remote_copy(
            src_ref=src, dst_ref=dst, send_sem=ss, recv_sem=rs, device_id=device, device_id_type=MESH
        )

    barrier = pltpu.get_barrier_semaphore()
    for d in order:
        pl.semaphore_signal(barrier, inc=1, device_id=(r ^ d, c), device_id_type=MESH)
    for d in range(1, n_col):
        pl.semaphore_signal(barrier, inc=1, device_id=(r, (c + d) % n_col), device_id_type=MESH)

    pivot_copy = pltpu.make_async_copy(pivot_hbm, weights.at[pl.ds(0, rows)], weight_sem.at[0])
    factor_copy = pltpu.make_async_copy(factor_hbm, weights.at[pl.ds(rows, rows)], weight_sem.at[1])
    pivot_copy.start()
    factor_copy.start()

    lane = lax.broadcasted_iota(jnp.int32, (8, 128), 1)
    targets = [target_ref[g] for g in range(held)]

    def chosen(peer):
        first, last = jnp.int32(held), jnp.int32(-1)
        slot_first, slot_last = jnp.int32(-1), jnp.int32(-1)
        for g in range(held):
            match = lax.div(targets[g], held) == peer
            fresh = jnp.logical_and(match, last < 0)
            first = jnp.where(fresh, g, first)
            slot_first = jnp.where(fresh, lax.rem(targets[g], held), slot_first)
            last = jnp.where(match, g, last)
            slot_last = jnp.where(match, lax.rem(targets[g], held), slot_last)
        message = jnp.where(lane == 0, slot_first, slot_last)
        return jnp.minimum(first, held - 1), jnp.maximum(last, 0), message

    def data_copy(n, d):
        return remote(
            staging.at[n], arrived.at[pl.ds(r * CAP, CAP)], send.at[n], recv.at[n], (r ^ d, c)
        )

    def slot_copy(n, d):
        return remote(messages.at[n], slots.at[r], send_int.at[n], recv_int.at[n], (r ^ d, c))

    picks = []
    for n, d in enumerate(order):
        first, last, messages[n] = chosen(r ^ d)
        picks.append((first, last))
        staging[n, 0] = rhs_ref[first]
        staging[n, 1] = rhs_ref[last]
        if n == 0:
            pl.semaphore_wait(barrier, n_row + n_col - 2)
        slot_copy(n, d).start()
        data_copy(n, d).start()
    first, last, slots[r] = chosen(r)
    arrived[r * CAP] = rhs_ref[first]
    arrived[r * CAP + 1] = rhs_ref[last]

    for n, d in enumerate(order):
        slot_copy(n, d).wait_recv()
    to_smem = pltpu.make_async_copy(slots, slots_smem, slot_sem)
    to_smem.start()
    to_smem.wait()
    found = [slots_smem[s, 0, rank] for s in range(n_row) for rank in range(CAP)]
    for b in range(held):
        place = jnp.int32(0)
        for j, slot in enumerate(found):
            place = jnp.where(slot == b, j, place)
        place_ref[b] = place

    pivot_copy.wait()
    factor_copy.wait()
    for n, d in enumerate(order):
        data_copy(n, d).wait_recv()

    for b in range(half):
        part = pl.ds(b * BLK, BLK)
        high[part], low[part] = split(arrived[place_ref[b]])
    for start in range(0, rows, tile):
        deep = start + tile
        solved[start : start + tile] = dot3(weights[start : start + tile, :deep], high[:deep], low[:deep])
    for start in range(0, rows, tile):
        part = pl.ds(start, tile)
        high[part], low[part] = split(solved[part])
    for start in range(0, rows, tile):
        value = dot3(weights[rows + start : rows + start + tile], high[:rows], low[:rows])
        for step in range(tile // BLK):
            b = start // BLK + step
            updated[b] = arrived[place_ref[half + b]] - value[step * BLK : (step + 1) * BLK]

    deep = min(rows, size)
    inverse_copies = [
        pltpu.make_async_copy(
            inverse_hbm.at[:, pl.ds(n * deep, deep)],
            weights.at[pl.ds(n * n_col * BLK, n_col * BLK), pl.ds(0, deep)],
            weight_sem.at[n],
        )
        for n in range(size // deep)
    ]
    for copy in inverse_copies:
        copy.start()

    def rows_of(i):
        return pl.ds(pl.multiple_of(i * step_rows, step_rows), step_rows)

    per_block = BLK // step_rows
    maps = [map_ref[b] for b in range(half)]

    def dense(column, i):
        block = column * n_row + i // per_block
        part = pl.ds(pl.multiple_of((i % per_block) * step_rows, step_rows), step_rows)
        value = None
        for b in range(half):
            term = updated[b, part] * jnp.where(maps[b] == block, 1.0, 0.0)
            value = term if value is None else value + term
        return value

    partner = (r, c - k + (1 - k))

    def core_copy(d, i):
        return remote(
            give.at[d, rows_of(i)], got_core.at[d, rows_of(i)], core_send.at[d], core_recv.at[d, i], partner
        )

    def x_copy(d, i):
        return remote(
            got_core.at[d, rows_of(i)],
            got_x.at[d - 1, rows_of(i)],
            x_send.at[d - 1],
            x_recv.at[d - 1, i],
            (r, ((x + d) % n_x) * 2 + k),
        )

    def stage_core(i):
        for d in range(n_x - 1, -1, -1):
            give[d, rows_of(i)] = dense(2 * ((x + d) % n_x) + (1 - k), i)
            core_copy(d, i).start()

    def stage_x(i):
        for d in range(n_x - 1, -1, -1):
            value = dense(2 * ((x + d) % n_x) + k, i)
            core_copy(d, i).wait_recv()
            got_core[d, rows_of(i)] = value + got_core[d, rows_of(i)]
            if d:
                x_copy(d, i).start()

    def join_x(i):
        value = base[rows_of(i)]
        for d in range(1, n_x):
            x_copy(d, i).wait_recv()
            value = value + got_x[d - 1, rows_of(i)]
        base[rows_of(i)] = value

    def line(n, pos, stride, own, up, down, ds, ss, rs):
        def send_up(i, source):
            return remote(source.at[rows_of(i)], up.at[rows_of(i)], ss.at[0], rs.at[0, i], (r + stride, c))

        def send_down(i, source):
            return remote(source.at[rows_of(i)], down.at[rows_of(i)], ss.at[1], rs.at[1, i], (r - stride, c))

        def hop(h, i):
            for place, landed, total, go in (
                (pos, up, up, send_up),
                (n - 1 - pos, down, ds, send_down),
            ):
                @pl.when(place == h)
                def _():
                    if h == 0:
                        go(i, own).start()
                    else:
                        go(i, total).wait_recv()
                        if h < n - 1:
                            total[rows_of(i)] = own[rows_of(i)] + landed[rows_of(i)]
                            go(i, total).start()

        def total(i, write):
            part = rows_of(i)

            @pl.when(pos == 0)
            def _():
                write(part, own[part] + down[part])

            @pl.when(pos == n - 1)
            def _():
                write(part, own[part] + up[part])

            if n > 2:
                @pl.when(jnp.logical_and(pos > 0, pos < n - 1))
                def _():
                    write(part, up[part] + down[part])

        def drain():
            whole = pl.ds(0, size)

            @pl.when(pos < n - 1)
            def _():
                remote(own.at[whole], up.at[whole], ss.at[0], rs.at[0, 0], (r + stride, c)).wait_send()

            @pl.when(pos > 0)
            def _():
                remote(own.at[whole], down.at[whole], ss.at[1], rs.at[1, 0], (r - stride, c)).wait_send()

        return hop, total, drain

    y_hop, y_total, y_drain = line(n_y, y, 1, base, y_up, y_down, y_ds, y_send, y_recv)
    z_hop, z_total, z_drain = line(n_z, z, n_y, mid, z_up, z_down, z_ds, z_send, z_recv)

    def write_mid(part, value):
        mid[part] = value

    def write_split(part, value):
        high[part], low[part] = split(value)

    def y_first(i):
        join_x(i)
        y_hop(0, i)

    def z_first(i):
        y_hop(n_y - 1, i)
        y_total(i, write_mid)
        z_hop(0, i)

    def z_last(i):
        z_hop(n_z - 1, i)
        z_total(i, write_split)

    at = CORE_SKEW + LEAD
    stages = [(0, stage_core), (CORE_SKEW, stage_x), (at, y_first)]
    for h in range(1, n_y - 1):
        at += SKEW
        stages.append((at, functools.partial(y_hop, h)))
    at += SKEW
    stages.append((at, z_first))
    for h in range(1, n_z - 1):
        at += SKEW
        stages.append((at, functools.partial(z_hop, h)))
    at += SKEW
    stages.append((at, z_last))

    @pl.loop(0, CHUNKS + at)
    def _(t):
        for offset, stage in stages:
            i = t - offset

            @pl.when(jnp.logical_and(i >= 0, i < CHUNKS))
            def _():
                stage(i)

    for copy in inverse_copies:
        copy.wait()
    for start in range(0, n_col * BLK, tile):
        value = None
        for n in range(size // deep):
            part = slice(n * deep, (n + 1) * deep)
            at_row = n * n_col * BLK + start
            term = dot3(weights[at_row : at_row + tile, :deep], high[part], low[part])
            value = term if value is None else value + term
        product[start : start + tile] = value

    def col_copy(d):
        to = (c + d) % n_col
        return remote(
            product.at[pl.ds(pl.multiple_of(to * BLK, BLK), BLK)],
            got_col.at[d - 1],
            col_send.at[d - 1],
            col_recv.at[d - 1],
            (r, to),
        )

    for d in range(1, n_col):
        col_copy(d).start()
    value = product[pl.ds(pl.multiple_of(c * BLK, BLK), BLK)]
    for d in range(1, n_col):
        col_copy(d).wait_recv()
        value = value + got_col[d - 1]
    out[...] = value

    for n, d in enumerate(order):
        slot_copy(n, d).wait_send()
        data_copy(n, d).wait_send()
    for d in range(1, n_col):
        col_copy(d).wait_send()
    for d in range(n_x):
        remote(give.at[d], got_core.at[d], core_send.at[d], core_recv.at[d, 0], partner).wait_send()
    for d in range(1, n_x):
        remote(
            got_core.at[d], got_x.at[d - 1], x_send.at[d - 1], x_recv.at[d - 1, 0],
            (r, ((x + d) % n_x) * 2 + k),
        ).wait_send()
    y_drain()
    z_drain()


def shards(rhs, block_target, pivot_inverse, update_factor, root_inverse, update_map):
    n_row, n_col = lax.axis_size("row"), lax.axis_size("col")
    n_x = n_col // 2
    width = rhs.shape[1]
    held = rhs.shape[0] // BLK
    rows = pivot_inverse.shape[0]
    size = n_row * BLK
    f32 = jnp.float32
    half = n_row // 2
    near = list(range(half - 1, 1, -1))
    cross = list(range(n_row - 1, half - 1, -1))
    order = []
    for n in range(max(len(near), len(cross))):
        order += near[n : n + 1] + cross[n : n + 1]
    order += [1]
    slab = pltpu.VMEM((size, width), f32)
    longest = max(rows, size)
    dma = pltpu.SemaphoreType.DMA
    return pl.pallas_call(
        functools.partial(forward_kernel, n_row, n_col, order),
        out_shape=(
            jax.ShapeDtypeStruct((rows, width), f32),
            jax.ShapeDtypeStruct((BLK, width), f32),
        ),
        in_specs=[SMEM, SMEM, VMEM, ANY, ANY, ANY],
        out_specs=(VMEM, VMEM),
        scratch_shapes=[
            pltpu.VMEM((n_row - 1, CAP, BLK, width), f32),
            pltpu.VMEM((n_row - 1, 8, 128), jnp.int32),
            pltpu.VMEM((n_row * CAP, BLK, width), f32),
            pltpu.VMEM((n_row, 8, 128), jnp.int32),
            pltpu.SMEM((n_row, 8, 128), jnp.int32),
            pltpu.SMEM((held,), jnp.int32),
            pltpu.VMEM((2 * rows, rows), f32),
            pltpu.VMEM((longest, width), jnp.bfloat16),
            pltpu.VMEM((longest, width), jnp.bfloat16),
            pltpu.VMEM((rows // BLK, BLK, width), f32),
            pltpu.VMEM((n_x, size, width), f32),
            pltpu.VMEM((n_x, size, width), f32),
            pltpu.VMEM((n_x - 1, size, width), f32),
        ]
        + [slab] * 7
        + [
            pltpu.VMEM((n_col * BLK, width), f32),
            pltpu.VMEM((n_col - 1, BLK, width), f32),
            dma((2,)),
            dma(()),
        ]
        + [dma((n_row - 1,))] * 4
        + [
            dma((n_x,)),
            dma((n_x, CHUNKS)),
            dma((n_x - 1,)),
            dma((n_x - 1, CHUNKS)),
            dma((2,)),
            dma((2, CHUNKS)),
            dma((2,)),
            dma((2, CHUNKS)),
            dma((n_col - 1,)),
            dma((n_col - 1,)),
        ],
        compiler_params=pltpu.CompilerParams(
            collective_id=0, has_side_effects=True, vmem_limit_bytes=67043328
        ),
        name="forward",
    )(block_target, update_map, rhs.reshape(held, BLK, width), pivot_inverse, update_factor, root_inverse)


def solution(mesh):
    return jax.shard_map(
        shards,
        mesh=mesh,
        in_specs=(
            P(("row", "col"), None),
            P(("row", "col")),
            P(("row", "col"), None),
            P(("row", "col"), None),
            P("row", "col"),
            P(("row", "col")),
        ),
        out_specs=(P(("row", "col"), None), P(("row", "col"), None)),
        check_vma=False,
    )
```

time: 125 us -> 114 us (0.912)
  Pallas kernels: 123 us -> 109 us
  local copies, waits for them, and re-layouts: 1.57 us -> 3.83 us
    pallas_call x3 -> x1, Pallas kernels: 123 us -> 109 us  [shards(): pl.pallas_call(functools.partial(forward_kernel, n_row, n_col, order), ou...]
    unnamed x1 -> x2, local copies, waits for them, and re-layouts: 1.57 us -> 3.83 us
where the time goes in v2:
time: 114 us
  Pallas kernels  109 us (96%)
  local copies, waits for them, and re-layouts  3.83 us (3%)
    pallas_call x1, Pallas kernels, shards(): pl.pallas_call(functools.partial(forward_kernel, n_row, n_col, order), ou...  109 us
    unnamed x2, local copies, waits for them, and re-layouts  3.83 us

profile of v2, /device:TPU:1, one launch (start us, length us, event | category | flops | bytes accessed | tf_op | source)
XLA Modules:
  0.0 113.6 jit_solution(16642488529638045256)
XLA Ops:
  0.6 109.1 %forward.1 = (f32[1024,256]{1,0:T(8,128)}, f32[128,256]{1,0:T(8,128)}) custom-call(s32[16]{0:T(128)} %target_ref.1, s32[8]{0:T(128)} %map_ref.1, f32[16,128,256]{2,1,0:T(8,128)} %bitcast.1, f32[1024,1024]{1,0:T(8,128)} %pivot_hbm.1, f32[1024,1024]{1,0:T(8,128)} %factor_hbm.1, f32[512,1024]{1,0:T(8,128)} %inverse_hbm.1), custom_call_target="tpu_custom_call" | custom-call | tf_op jit(solution)/shard_map/forward/pallas_call | solution.py:361
  109.8 2.3 %copy.10 = f32[1024,256]{1,0:T(8,128)} copy(f32[1024,256]{1,0:T(8,128)} %get-tuple-element.4) | data formatting | bytes 2097152
  112.0 1.6 %copy.11 = f32[128,256]{1,0:T(8,128)} copy(f32[128,256]{1,0:T(8,128)} %get-tuple-element.5) | data formatting | bytes 262144

commit v3 on v2

v3 whole, which is shorter than its diff:
```python
import functools
import jax
import jax.numpy as jnp
from jax import lax
from jax.experimental import pallas as pl
from jax.experimental.pallas import tpu as pltpu
from jax.sharding import PartitionSpec as P

BLK = 128
CAP = 2
PARTS = 2
CHUNKS = 16
CORE_SKEW = 2
LEAD = 6
SKEW = 4
MESH = pl.DeviceIdType.MESH
VMEM = pl.BlockSpec(memory_space=pltpu.VMEM)
SMEM = pl.BlockSpec(memory_space=pltpu.SMEM)
ANY = pl.BlockSpec(memory_space=pl.ANY)


def split(value):
    high = value.astype(jnp.bfloat16)
    low = (value - high.astype(jnp.float32)).astype(jnp.bfloat16)
    return high, low


def dot3(a, b_high, b_low):
    a_high, a_low = split(a)
    total = jnp.dot(a_high, b_low, preferred_element_type=jnp.float32)
    total += jnp.dot(a_low, b_high, preferred_element_type=jnp.float32)
    return total + jnp.dot(a_high, b_high, preferred_element_type=jnp.float32)


def forward_kernel(
    n_row, n_col, order, target_ref, map_ref, rhs_ref, pivot_hbm, factor_hbm, inverse_hbm,
    solved, out,
    staging, messages, arrived_a, arrived_b, slots, slots_smem, place_ref, weights, high, low, updated,
    give, got_core, got_x, y_up, y_down, y_ds, mid, z_up, z_down, z_ds, product, got_col,
    weight_sem, slot_sem, send, recv, send_int, recv_int,
    core_send, core_recv, x_send, x_recv, y_send, y_recv, z_send, z_recv, col_send, col_recv,
):
    n_y = max(1, n_col // 2)
    n_z, n_x = n_row // n_y, n_col // 2
    r, c = lax.axis_index("row"), lax.axis_index("col")
    z, y, x, k = r // n_y, r % n_y, c // 2, c % 2
    size = n_row * BLK
    step_rows = size // CHUNKS
    held = rhs_ref.shape[0]
    rows = solved.shape[0]
    half = rows // BLK
    tile = 2 * BLK
    base = got_core.at[0]
    arrived = (arrived_a, arrived_b)
    lanes = solved.shape[1] // PARTS

    def cols(h):
        return pl.ds(h * lanes, lanes)


    def remote(src, dst, ss, rs, device):
        return pltpu.make_async_remote_copy(
            src_ref=src, dst_ref=dst, send_sem=ss, recv_sem=rs, device_id=device, device_id_type=MESH
        )

    barrier = pltpu.get_barrier_semaphore()
    for d in order:
        pl.semaphore_signal(barrier, inc=1, device_id=(r ^ d, c), device_id_type=MESH)
    for d in range(1, n_col):
        pl.semaphore_signal(barrier, inc=1, device_id=(r, (c + d) % n_col), device_id_type=MESH)

    pivot_copy = pltpu.make_async_copy(pivot_hbm, weights.at[pl.ds(0, rows)], weight_sem.at[0])
    factor_copy = pltpu.make_async_copy(factor_hbm, weights.at[pl.ds(rows, rows)], weight_sem.at[1])
    pivot_copy.start()
    factor_copy.start()

    lane = lax.broadcasted_iota(jnp.int32, (8, 128), 1)
    targets = [target_ref[g] for g in range(held)]

    def chosen(peer):
        first, last = jnp.int32(held), jnp.int32(-1)
        slot_first, slot_last = jnp.int32(-1), jnp.int32(-1)
        for g in range(held):
            match = lax.div(targets[g], held) == peer
            fresh = jnp.logical_and(match, last < 0)
            first = jnp.where(fresh, g, first)
            slot_first = jnp.where(fresh, lax.rem(targets[g], held), slot_first)
            last = jnp.where(match, g, last)
            slot_last = jnp.where(match, lax.rem(targets[g], held), slot_last)
        message = jnp.where(lane == 0, slot_first, slot_last)
        return jnp.minimum(first, held - 1), jnp.maximum(last, 0), message

    def data_copy(n, d, h):
        return remote(
            staging.at[n, :, :, cols(h)],
            arrived[h].at[pl.ds(r * CAP, CAP)],
            send.at[h, n],
            recv.at[h, n],
            (r ^ d, c),
        )

    def slot_copy(n, d):
        return remote(messages.at[n], slots.at[r], send_int.at[n], recv_int.at[n], (r ^ d, c))

    picks = []
    for n, d in enumerate(order):
        first, last, messages[n] = chosen(r ^ d)
        picks.append((first, last))
        staging[n, 0] = rhs_ref[first]
        staging[n, 1] = rhs_ref[last]
        if n == 0:
            pl.semaphore_wait(barrier, n_row + n_col - 2)
        slot_copy(n, d).start()
        data_copy(n, d, 0).start()
    for h in range(1, PARTS):
        for n, d in enumerate(order):
            data_copy(n, d, h).start()
    first, last, slots[r] = chosen(r)
    for h in range(PARTS):
        arrived[h][r * CAP] = rhs_ref[first, :, cols(h)]
        arrived[h][r * CAP + 1] = rhs_ref[last, :, cols(h)]

    for n, d in enumerate(order):
        slot_copy(n, d).wait_recv()
    to_smem = pltpu.make_async_copy(slots, slots_smem, slot_sem)
    to_smem.start()
    to_smem.wait()
    found = [slots_smem[s, 0, rank] for s in range(n_row) for rank in range(CAP)]
    for b in range(held):
        place = jnp.int32(0)
        for j, slot in enumerate(found):
            place = jnp.where(slot == b, j, place)
        place_ref[b] = place

    pivot_copy.wait()
    factor_copy.wait()
    def front(h):
        for n, d in enumerate(order):
            data_copy(n, d, h).wait_recv()
        for b in range(half):
            part = pl.ds(b * BLK, BLK)
            high[part, cols(h)], low[part, cols(h)] = split(arrived[h][place_ref[b]])
        for start in range(0, rows, tile):
            deep = start + tile
            solved[start : start + tile, cols(h)] = dot3(
                weights[start : start + tile, :deep], high[:deep, cols(h)], low[:deep, cols(h)]
            )
        for start in range(0, rows, tile):
            part = pl.ds(start, tile)
            high[part, cols(h)], low[part, cols(h)] = split(solved[part, cols(h)])
        for start in range(0, rows, tile):
            value = dot3(
                weights[rows + start : rows + start + tile], high[:rows, cols(h)], low[:rows, cols(h)]
            )
            for step in range(tile // BLK):
                b = start // BLK + step
                updated[b, :, cols(h)] = (
                    arrived[h][place_ref[half + b]] - value[step * BLK : (step + 1) * BLK]
                )

    deep = min(rows, size)
    inverse_copies = [
        pltpu.make_async_copy(
            inverse_hbm.at[:, pl.ds(n * deep, deep)],
            weights.at[pl.ds(n * n_col * BLK, n_col * BLK), pl.ds(0, deep)],
            weight_sem.at[n],
        )
        for n in range(size // deep)
    ]
    def rows_of(i):
        return pl.ds(pl.multiple_of(i * step_rows, step_rows), step_rows)

    per_block = BLK // step_rows
    maps = [map_ref[b] for b in range(half)]

    partner = (r, c - k + (1 - k))

    def root(h):
        def dense(column, i):
            block = column * n_row + i // per_block
            part = pl.ds(pl.multiple_of((i % per_block) * step_rows, step_rows), step_rows)
            value = None
            for b in range(half):
                term = updated[b, part, cols(h)] * jnp.where(maps[b] == block, 1.0, 0.0)
                value = term if value is None else value + term
            return value

        def core_copy(d, i):
            return remote(
                give.at[d, rows_of(i), cols(h)], got_core.at[d, rows_of(i), cols(h)], core_send.at[h, d], core_recv.at[h, d, i], partner
            )

        def x_copy(d, i):
            return remote(
                got_core.at[d, rows_of(i), cols(h)],
                got_x.at[d - 1, rows_of(i), cols(h)],
                x_send.at[h, d - 1],
                x_recv.at[h, d - 1, i],
                (r, ((x + d) % n_x) * 2 + k),
            )

        def stage_core(i):
            for d in range(n_x - 1, -1, -1):
                give[d, rows_of(i), cols(h)] = dense(2 * ((x + d) % n_x) + (1 - k), i)
                core_copy(d, i).start()

        def stage_x(i):
            for d in range(n_x - 1, -1, -1):
                value = dense(2 * ((x + d) % n_x) + k, i)
                core_copy(d, i).wait_recv()
                got_core[d, rows_of(i), cols(h)] = value + got_core[d, rows_of(i), cols(h)]
                if d:
                    x_copy(d, i).start()

        def join_x(i):
            value = base[rows_of(i), cols(h)]
            for d in range(1, n_x):
                x_copy(d, i).wait_recv()
                value = value + got_x[d - 1, rows_of(i), cols(h)]
            base[rows_of(i), cols(h)] = value

        def line(n, pos, stride, own, up, down, ds, ss, rs):
            def send_up(i, source):
                return remote(source.at[rows_of(i), cols(h)], up.at[rows_of(i), cols(h)], ss.at[h, 0], rs.at[h, 0, i], (r + stride, c))

            def send_down(i, source):
                return remote(source.at[rows_of(i), cols(h)], down.at[rows_of(i), cols(h)], ss.at[h, 1], rs.at[h, 1, i], (r - stride, c))

            def hop(step, i):
                for place, landed, total, go in (
                    (pos, up, up, send_up),
                    (n - 1 - pos, down, ds, send_down),
                ):
                    @pl.when(place == step)
                    def _():
                        if step == 0:
                            go(i, own).start()
                        else:
                            go(i, total).wait_recv()
                            if step < n - 1:
                                total[rows_of(i), cols(h)] = own[rows_of(i), cols(h)] + landed[rows_of(i), cols(h)]
                                go(i, total).start()

            def total(i, write):
                part = rows_of(i)

                @pl.when(pos == 0)
                def _():
                    write(part, own[part, cols(h)] + down[part, cols(h)])

                @pl.when(pos == n - 1)
                def _():
                    write(part, own[part, cols(h)] + up[part, cols(h)])

                if n > 2:
                    @pl.when(jnp.logical_and(pos > 0, pos < n - 1))
                    def _():
                        write(part, up[part, cols(h)] + down[part, cols(h)])

            def drain():
                whole = pl.ds(0, size)

                @pl.when(pos < n - 1)
                def _():
                    remote(own.at[whole, cols(h)], up.at[whole, cols(h)], ss.at[h, 0], rs.at[h, 0, 0], (r + stride, c)).wait_send()

                @pl.when(pos > 0)
                def _():
                    remote(own.at[whole, cols(h)], down.at[whole, cols(h)], ss.at[h, 1], rs.at[h, 1, 0], (r - stride, c)).wait_send()

            return hop, total, drain

        y_hop, y_total, y_drain = line(n_y, y, 1, base, y_up, y_down, y_ds, y_send, y_recv)
        z_hop, z_total, z_drain = line(n_z, z, n_y, mid, z_up, z_down, z_ds, z_send, z_recv)

        def write_mid(part, value):
            mid[part, cols(h)] = value

        def write_split(part, value):
            high[part, cols(h)], low[part, cols(h)] = split(value)

        def y_first(i):
            join_x(i)
            y_hop(0, i)

        def z_first(i):
            y_hop(n_y - 1, i)
            y_total(i, write_mid)
            z_hop(0, i)

        def z_last(i):
            z_hop(n_z - 1, i)
            z_total(i, write_split)

        def drain():
            for d in range(n_x):
                remote(
                    give.at[d, :, cols(h)], got_core.at[d, :, cols(h)],
                    core_send.at[h, d], core_recv.at[h, d, 0], partner,
                ).wait_send()
            for d in range(1, n_x):
                remote(
                    got_core.at[d, :, cols(h)], got_x.at[d - 1, :, cols(h)],
                    x_send.at[h, d - 1], x_recv.at[h, d - 1, 0],
                    (r, ((x + d) % n_x) * 2 + k),
                ).wait_send()
            y_drain()
            z_drain()

        at = CORE_SKEW + LEAD
        head = [(0, stage_core), (CORE_SKEW, stage_x), (at, y_first)]
        for step in range(1, n_y - 1):
            at += SKEW
            head.append((at, functools.partial(y_hop, step)))
        head.append((at + SKEW, z_first))
        tail = [((step - 1) * SKEW, functools.partial(z_hop, step)) for step in range(1, n_z - 1)]
        tail.append(((n_z - 2) * SKEW, z_last))
        return head, tail, drain

    def run(stages):
        @pl.loop(0, CHUNKS + max(offset for offset, _ in stages))
        def _(t):
            for offset, stage in stages:
                i = t - offset

                @pl.when(jnp.logical_and(i >= 0, i < CHUNKS))
                def _():
                    stage(i)

    parts = [root(h) for h in range(PARTS)]
    left = []
    for h, (head, tail, _) in enumerate(parts):
        front(h)
        if h == PARTS - 1:
            for copy in inverse_copies:
                copy.start()
            after = max(offset for offset, _ in head) + SKEW
            tail = [(after + offset, stage) for offset, stage in tail]
            run(left + head + tail)
        else:
            run(left + head)
            left = tail

    for copy in inverse_copies:
        copy.wait()
    for start in range(0, n_col * BLK, tile):
        value = None
        for n in range(size // deep):
            part = slice(n * deep, (n + 1) * deep)
            at_row = n * n_col * BLK + start
            term = dot3(weights[at_row : at_row + tile, :deep], high[part], low[part])
            value = term if value is None else value + term
        product[start : start + tile] = value

    def col_copy(d):
        to = (c + d) % n_col
        return remote(
            product.at[pl.ds(pl.multiple_of(to * BLK, BLK), BLK)],
            got_col.at[d - 1],
            col_send.at[d - 1],
            col_recv.at[d - 1],
            (r, to),
        )

    for d in range(1, n_col):
        col_copy(d).start()
    value = product[pl.ds(pl.multiple_of(c * BLK, BLK), BLK)]
    for d in range(1, n_col):
        col_copy(d).wait_recv()
        value = value + got_col[d - 1]
    out[...] = value

    for n, d in enumerate(order):
        slot_copy(n, d).wait_send()
        for h in range(PARTS):
            data_copy(n, d, h).wait_send()
    for d in range(1, n_col):
        col_copy(d).wait_send()
    for _, _, drain in parts:
        drain()


def shards(rhs, block_target, pivot_inverse, update_factor, root_inverse, update_map):
    n_row, n_col = lax.axis_size("row"), lax.axis_size("col")
    n_x = n_col // 2
    width = rhs.shape[1]
    held = rhs.shape[0] // BLK
    rows = pivot_inverse.shape[0]
    size = n_row * BLK
    f32 = jnp.float32
    half = n_row // 2
    near = list(range(half - 1, 1, -1))
    cross = list(range(n_row - 1, half - 1, -1))
    order = []
    for n in range(max(len(near), len(cross))):
        order += near[n : n + 1] + cross[n : n + 1]
    order += [1]
    slab = pltpu.VMEM((size, width), f32)
    longest = max(rows, size)
    dma = pltpu.SemaphoreType.DMA
    return pl.pallas_call(
        functools.partial(forward_kernel, n_row, n_col, order),
        out_shape=(
            jax.ShapeDtypeStruct((rows, width), f32),
            jax.ShapeDtypeStruct((BLK, width), f32),
        ),
        in_specs=[SMEM, SMEM, VMEM, ANY, ANY, ANY],
        out_specs=(VMEM, VMEM),
        scratch_shapes=[
            pltpu.VMEM((n_row - 1, CAP, BLK, width), f32),
            pltpu.VMEM((n_row - 1, 8, 128), jnp.int32),
            pltpu.VMEM((n_row * CAP, BLK, width // PARTS), f32),
            pltpu.VMEM((n_row * CAP, BLK, width // PARTS), f32),
            pltpu.VMEM((n_row, 8, 128), jnp.int32),
            pltpu.SMEM((n_row, 8, 128), jnp.int32),
            pltpu.SMEM((held,), jnp.int32),
            pltpu.VMEM((2 * rows, rows), f32),
            pltpu.VMEM((longest, width), jnp.bfloat16),
            pltpu.VMEM((longest, width), jnp.bfloat16),
            pltpu.VMEM((rows // BLK, BLK, width), f32),
            pltpu.VMEM((n_x, size, width), f32),
            pltpu.VMEM((n_x, size, width), f32),
            pltpu.VMEM((n_x - 1, size, width), f32),
        ]
        + [slab] * 7
        + [
            pltpu.VMEM((n_col * BLK, width), f32),
            pltpu.VMEM((n_col - 1, BLK, width), f32),
            dma((2,)),
            dma(()),
        ]
        + [dma((PARTS, n_row - 1))] * 2
        + [dma((n_row - 1,))] * 2
        + [
            dma((PARTS, n_x)),
            dma((PARTS, n_x, CHUNKS)),
            dma((PARTS, n_x - 1)),
            dma((PARTS, n_x - 1, CHUNKS)),
            dma((PARTS, 2)),
            dma((PARTS, 2, CHUNKS)),
            dma((PARTS, 2)),
            dma((PARTS, 2, CHUNKS)),
            dma((n_col - 1,)),
            dma((n_col - 1,)),
        ],
        compiler_params=pltpu.CompilerParams(
            collective_id=0, has_side_effects=True, vmem_limit_bytes=67043328
        ),
        name="forward",
    )(block_target, update_map, rhs.reshape(held, BLK, width), pivot_inverse, update_factor, root_inverse)


def solution(mesh):
    return jax.shard_map(
        shards,
        mesh=mesh,
        in_specs=(
            P(("row", "col"), None),
            P(("row", "col")),
            P(("row", "col"), None),
            P(("row", "col"), None),
            P("row", "col"),
            P(("row", "col")),
        ),
        out_specs=(P(("row", "col"), None), P(("row", "col"), None)),
        check_vma=False,
    )
```

time: 114 us -> 110 us (0.965)
  Pallas kernels: 109 us -> 105 us
    pallas_call x1, Pallas kernels: 109 us -> 105 us  [shards(): pl.pallas_call(functools.partial(forward_kernel, n_row, n_col, order), ou...]
where the time goes in v3:
time: 110 us
  Pallas kernels  105 us (95%)
  local copies, waits for them, and re-layouts  3.83 us (3%)
    pallas_call x1, Pallas kernels, shards(): pl.pallas_call(functools.partial(forward_kernel, n_row, n_col, order), ou...  105 us
    unnamed x2, local copies, waits for them, and re-layouts  3.83 us

profile of v3, /device:TPU:1, one launch (start us, length us, event | category | flops | bytes accessed | tf_op | source)
XLA Modules:
  0.0 109.6 jit_solution(12651599896767453615)
XLA Ops:
  0.6 105.2 %forward.1 = (f32[1024,256]{1,0:T(8,128)}, f32[128,256]{1,0:T(8,128)}) custom-call(s32[16]{0:T(128)} %target_ref.1, s32[8]{0:T(128)} %map_ref.1, f32[16,128,256]{2,1,0:T(8,128)} %bitcast.1, f32[1024,1024]{1,0:T(8,128)} %pivot_hbm.1, f32[1024,1024]{1,0:T(8,128)} %factor_hbm.1, f32[512,1024]{1,0:T(8,128)} %inverse_hbm.1), custom_call_target="tpu_custom_call" | custom-call | tf_op jit(solution)/shard_map/forward/pallas_call | solution.py:401
  105.8 2.3 %copy.10 = f32[1024,256]{1,0:T(8,128)} copy(f32[1024,256]{1,0:T(8,128)} %get-tuple-element.4) | data formatting | bytes 2097152
  108.1 1.6 %copy.11 = f32[128,256]{1,0:T(8,128)} copy(f32[128,256]{1,0:T(8,128)} %get-tuple-element.5) | data formatting | bytes 262144
